TPU v7x, 256 devices: a whole 4x4x8 slice. The times are simulated.
256 devices in a mesh: front: 32 (over z, x), panel: 8 (over y, core).
Axes of the slice: x: 4, y: 4, z: 8, core: 2. Of those that a mesh axis runs over, the one named last changes fastest.
Arguments:
- coupling: bfloat16 [32, 2048, 2048], P('front', 'panel'), may hold values from -1 to 1
- pivot_inverse: bfloat16 [32, 2048, 2048], P('front', 'panel'), may hold values from -0.125 to 0.125
- pivots: float32 [32, 2048], P('front'), as said below
- trailing: float32 [32, 2048, 2048], P('front', 'panel'), may hold values from -12 to 12
- sketch: float32 [32, 8, 8, 32, 256], P('front', 'panel'), may hold values from -6 to 6
- extend_map: int32 [32, 2048], replicated, may hold values from 0 to 511, as said below
- parent_of: int32 [32], replicated, may hold values from 0 to 31, as said below
- parent_base: bfloat16 [32, 4096, 4096], P('front', 'panel'), may hold values from -6 to 6
Outputs:
- assembled: bfloat16 [32, 4096, 4096], P('front', 'panel')
Inputs may be any that keep to these rules, and one draw needn't show every extreme that they name: `extend_map`: within each front and each aligned block of 2048 / 8 entries the values are distinct and rising. `pivots`: every entry's magnitude lies between 0.5 and 2 times 2048 ** -0.5; signs are mixed. `parent_of`: no parent has more than 4 children; some parent has exactly 4.
All inputs are finite; a program needn't handle non-finite values.
Results may differ from a plain program's by a relative error of at most 0.0043.
Values may be sent and summed in bfloat16 or wider, within the bound.
A program may use at most 128 MiB of HBM per device.

v0:
```python
import functools

import jax
import jax.numpy as jnp
from jax import lax
from jax.experimental import pallas as pl
from jax.experimental.pallas import tpu as pltpu
from jax.sharding import PartitionSpec as P

MAXKIDS = 4
HI = lax.Precision.HIGHEST


def dot(a, b, dims, precision=None):
    return lax.dot_general(
        a, b, (dims, ((), ())), precision=precision, preferred_element_type=jnp.float32
    )


def compress_kernel(schur_ref, omega_ref, basis_ref, coeff_ref):
    tiles, rank, tile = omega_ref.shape
    ys = []
    state = []
    row_id = lax.broadcasted_iota(jnp.int32, (rank, rank), 0)
    col_id = lax.broadcasted_iota(jnp.int32, (rank, rank), 1)
    eye = jnp.where(row_id == col_id, 1.0, 0.0).astype(jnp.float32)
    for j in range(tiles):
        block = schur_ref[:, j * tile:(j + 1) * tile]
        y = dot(omega_ref[j], block, ((1,), (1,)), HI)
        ys.append(y)
        state.append(jnp.concatenate([dot(y, y, ((1,), (1,)), HI), eye], axis=1))
    a = jnp.stack(state)
    rows = lax.broadcasted_iota(jnp.int32, (tiles, rank, 1), 1)
    for k in range(rank):
        pivot = a[:, k:k + 1, :]
        inverse = 1.0 / a[:, k:k + 1, k:k + 1]
        step = jnp.where(rows > k, a[:, :, k:k + 1] * inverse, 0.0)
        a = a - step * pivot
    for j in range(tiles):
        diag = jnp.sum(jnp.where(row_id == col_id, a[j, :, :rank], 0.0), axis=1, keepdims=True)
        inverse = a[j, :, rank:] * (1.0 / jnp.sqrt(diag))
        basis = dot(inverse, ys[j], ((1,), (0,)), HI)
        block = schur_ref[:, j * tile:(j + 1) * tile]
        basis_ref[j] = basis.astype(jnp.bfloat16)
        coeff_ref[j] = dot(basis, block, ((1,), (0,)), HI).astype(jnp.bfloat16)


def compress(schur, omega):
    tiles, rank, tile = omega.shape
    out = jax.ShapeDtypeStruct((tiles, rank, tile), jnp.bfloat16)
    return pl.pallas_call(
        compress_kernel,
        out_shape=(out, out),
        name="compress",
        compiler_params=pltpu.CompilerParams(vmem_limit_bytes=48 * 1024 * 1024),
    )(schur, omega)


def place_kernel(rowmap_ref, colmap_ref, basis_ref, coeff_ref, base_ref, out_ref, rt_ref):
    kids, _, tiles, rank, tile = basis_ref.shape
    height = out_ref.shape[1]
    width = out_ref.shape[2]
    j = pl.program_id(0)
    lanes = lax.broadcasted_iota(jnp.int32, (tile, width), 1)

    @pl.when(j == 0)
    def _():
        high = lax.broadcasted_iota(jnp.int32, (tile, height), 1)
        for s in range(kids):
            hot = jnp.where(rowmap_ref[:, s:s + 1] == high, 1.0, 0.0).astype(jnp.bfloat16)
            rt_ref[s] = dot(
                basis_ref[s, 0].reshape(tiles * rank, tile), hot, ((1,), (0,))
            ).astype(jnp.bfloat16)

    left = []
    right = []
    for s in range(kids):
        hot = jnp.where(colmap_ref[0, :, s:s + 1] == lanes, 1.0, 0.0).astype(jnp.bfloat16)
        right.append(dot(coeff_ref[s, 0, 0], hot, ((1,), (0,))).astype(jnp.bfloat16))
        left.append(rt_ref[s, pl.ds(j * rank, rank), :])
    left = jnp.concatenate(left, axis=0)
    right = jnp.concatenate(right, axis=0)
    total = dot(left, right, ((0,), (0,)))
    out_ref[0] = (base_ref[0].astype(jnp.float32) + total).astype(jnp.bfloat16)


def place(rowmap, colmap, data, base):
    kids, _, tiles, rank, tile = data.shape
    _, height, total = base.shape
    width = total // tiles
    return pl.pallas_call(
        place_kernel,
        grid=(tiles,),
        in_specs=[
            pl.BlockSpec((tile, kids), lambda j: (0, 0)),
            pl.BlockSpec((1, tile, kids), lambda j: (j, 0, 0)),
            pl.BlockSpec((kids, 1, tiles, rank, tile), lambda j: (0, 0, 0, 0, 0)),
            pl.BlockSpec((kids, 1, 1, rank, tile), lambda j: (0, 1, j, 0, 0)),
            pl.BlockSpec((1, height, width), lambda j: (0, 0, j)),
        ],
        out_specs=pl.BlockSpec((1, height, width), lambda j: (0, 0, j)),
        out_shape=jax.ShapeDtypeStruct(base.shape, base.dtype),
        scratch_shapes=[pltpu.VMEM((kids, tiles * rank, height), jnp.bfloat16)],
        name="place",
        compiler_params=pltpu.CompilerParams(vmem_limit_bytes=48 * 1024 * 1024),
    )(rowmap, colmap, data, data, base)


def family(parent_of):
    fronts = parent_of.shape[0]
    front_ids = jnp.arange(fronts, dtype=jnp.int32)
    same_parent = parent_of[:, None] == parent_of[None, :]
    position = jnp.sum(
        jnp.where(same_parent & (front_ids[None, :] < front_ids[:, None]), 1, 0), axis=1
    ).astype(jnp.int32)
    slot_ids = jnp.arange(MAXKIDS, dtype=jnp.int32)
    matches = (parent_of[None, :, None] == front_ids[:, None, None]) & (
        position[None, :, None] == slot_ids[None, None, :]
    )
    children = jnp.sum(jnp.where(matches, front_ids[None, :, None], 0), axis=1)
    present = jnp.any(matches, axis=1)
    return children, present


def body(coupling, pivot_inverse, pivots, trailing, sketch, extend_map, parent_of, parent_base):
    rows_here = coupling[0]
    row_dev = rows_here.shape[0]
    factor_sum = jnp.dot(
        rows_here,
        lax.all_gather(pivot_inverse, "panel", axis=1, tiled=True)[0],
        preferred_element_type=jnp.float32,
    )
    factor = factor_sum.astype(jnp.bfloat16)
    scaled = (factor.astype(jnp.float32) / pivots[0][None, :]).astype(jnp.bfloat16)
    gathered = lax.all_gather(factor, "panel", axis=0, tiled=True)
    update = dot(scaled, gathered, ((1,), (1,)))
    schur = trailing[0] - update
    basis, coeff = compress(schur, sketch[0, 0])

    panels = lax.axis_size("panel")
    owner = lax.axis_index("front")
    panel_here = lax.axis_index("panel")
    fronts = parent_of.shape[0]
    children, present = family(parent_of)
    packed = jnp.stack((basis, coeff)).reshape(fronts, -1)
    spread = lax.all_to_all(packed, "front", split_axis=0, concat_axis=0, tiled=True)
    chosen = jnp.take(spread, children.reshape(-1), axis=0)
    outgoing = jnp.where(present.reshape(-1)[:, None], chosen, jnp.zeros((), jnp.bfloat16)).reshape(
        fronts, MAXKIDS, -1
    )
    received = lax.all_to_all(outgoing, "front", split_axis=0, concat_axis=2, tiled=True)
    data = received[0].reshape((MAXKIDS, 2) + basis.shape)
    maps = jnp.where(present[owner][:, None], extend_map[children[owner]], -1)
    colmap = jnp.transpose(maps).reshape(panels, row_dev, MAXKIDS)
    rowmap = lax.dynamic_index_in_dim(colmap, panel_here, 0, keepdims=False)
    return place(rowmap, colmap, data, parent_base)


def solution(mesh):
    placed = (
        P("front", "panel", None),
        P("front", "panel", None),
        P("front", None),
        P("front", "panel", None),
        P("front", "panel", None, None, None),
        P(),
        P(),
        P("front", "panel", None),
    )
    return jax.shard_map(
        body, mesh=mesh, in_specs=placed, out_specs=P("front", "panel", None), check_vma=False
    )
```

profile of v0, /device:TPU:2, one launch (start us, length us, event | category | flops | bytes accessed | tf_op | source)
XLA Modules:
  0.0 220.4 jit_solution(16241216103105887888)
XLA Ops:
  6.5 0.7 all-gather.3.cloned.1.call-update
  7.3 57.1 %all-gather.3.cloned.1.call-done = bf16[1,2048,2048]{2,1,0:T(8,128)(2,1)} async-done(((bf16[1,256,2048]{2,1,0:T(8,128)(2,1)}), bf16[1,2048,2048]{2,1,0:T(8,128)(2,1)}) %all-gather.3.cloned.1.call-update) | async-done | bytes 8388624 | tf_op jit(solution)/shard_map/all_gather | solution.py:130
  64.4 6.7 %fusion.2 = bf16[256,2048]{1,0:T(8,128)(2,1)} fusion(bf16[1,2048,2048]{2,1,0:T(8,128)(2,1)} %all-gather.3.cloned.1.call-done, bf16[1,256,2048]{2,1,0:T(8,128)(2,1)S(1)} %copy-done), kind=kOutput, calls=%fused_computation.5 | convolution fusion | flops 2148007936 | bytes 10485760 | tf_op jit(solution)/shard_map/dot_general | solution.py:128
  71.1 0.2 select_reduce_fusion
  71.3 0.2 and_reduce_fusion
  71.5 0.1 copy.30
  71.6 0.2 fusion.7
  71.8 51.8 %all-gather.5.cloned.1.call-done = bf16[2048,2048]{1,0:T(8,128)(2,1)} async-done(((bf16[256,2048]{1,0:T(8,128)(2,1)}), bf16[2048,2048]{1,0:T(8,128)(2,1)}) %all-gather.5.cloned.1.call-update) | async-done | bytes 8388624 | tf_op jit(solution)/shard_map/all_gather | solution.py:135
  123.7 6.2 %convolution_subtract_fusion.schur_ref = f32[256,2048]{1,0:T(8,128)S(1)} fusion(bf16[2048,2048]{1,0:T(8,128)(2,1)} %all-gather.5.cloned.1.call-done, f32[1,256,2048]{2,1,0:T(8,128)S(1)} %copy-done.4, bf16[256,2048]{1,0:T(8,128)(2,1)} %fusion.2, f32[2048]{0:T(1024)S(1)} %bitcast.43), kind=kOutput, calls=%fused_computation.4 | convolution fusion | flops 2149580800 | bytes 13639680 | tf_op jit(solution)/shard_map/dot_general | solution.py:15
  129.9 8.6 %compress.1 = (bf16[8,32,256]{2,1,0:T(8,128)(2,1)S(1)}, bf16[8,32,256]{2,1,0:T(8,128)(2,1)S(1)}) custom-call(f32[256,2048]{1,0:T(8,128)S(1)} %convolution_subtract_fusion.schur_ref, f32[8,32,256]{2,1,0:T(8,128)S(1)} %bitcast.38), custom_call_target="tpu_custom_call" | custom-call | tf_op jit(solution)/shard_map/compress/pallas_call | solution.py:51
  138.5 0.1 all_to_all.25
  138.6 0.5 broadcast.104
  139.2 2.3 %reduce.4 = bf16[32,4096]{1,0:T(8,128)(2,1)S(1)} reduce(bf16[32,1,4096]{2,1,0:T(2,128)(2,1)S(1)} %all_to_all.25, bf16[]{:T(256)} %broadcast.104), dimensions={1}, to_apply=%all_to_all.25.reduce_sub_computation | reduce | bytes 524290 | tf_op jit(solution)/shard_map/all_to_all | solution.py:146
  141.4 0.9 reshape.152
  142.3 10.1 %all-to-all-start = ((bf16[32,2,2048]{2,1,0:T(2,128)(2,1)}), bf16[32,2,2048]{2,1,0:T(2,128)(2,1)S(1)}, u32[]{:S(2)}, u32[]{:S(2)}) async-start(bf16[32,2,2048]{2,1,0:T(2,128)(2,1)} %reshape.152), calls=%async_computation | async-start | bytes 524288 | tf_op jit(solution)/shard_map/all_to_all | solution.py:146
  152.5 0.1 copy.31
  152.6 0.1 reshape.133
  152.7 11.4 %all-to-all-done = bf16[32,2,2048]{2,1,0:T(2,128)(2,1)S(1)} async-done(((bf16[32,2,2048]{2,1,0:T(2,128)(2,1)}), bf16[32,2,2048]{2,1,0:T(2,128)(2,1)S(1)}, u32[]{:S(2)}, u32[]{:S(2)}) %all-to-all-start) | async-done | bytes 262176 | tf_op jit(solution)/shard_map/all_to_all | solution.py:146
  164.1 0.3 reshape.153
  164.4 0.3 copy.37
  164.7 1.2 gather_fusion.1
  165.9 0.4 gather.11
  166.3 1.7 select_select_fusion
  168.0 5.6 %all-to-all-start.1 = ((bf16[32,4,4096]{2,1,0:T(4,128)(2,1)}), bf16[32,4,4096]{2,1,0:T(4,128)(2,1)S(1)}, u32[]{:S(2)}, u32[]{:S(2)}) async-start(bf16[32,4,4096]{2,1,0:T(4,128)(2,1)} %select_select_fusion), calls=%async_computation.1 | async-start | bytes 2097152 | tf_op jit(solution)/shard_map/all_to_all | solution.py:151
  173.6 0.2 dynamic-slice_reduce_fusion
  173.8 0.2 dynamic-slice_reduce_fusion.1
  174.0 0.6 gather_fusion
  174.7 0.4 copy.29
  175.1 26.0 %all-to-all-done.1 = bf16[32,4,4096]{2,1,0:T(4,128)(2,1)S(1)} async-done(((bf16[32,4,4096]{2,1,0:T(4,128)(2,1)}), bf16[32,4,4096]{2,1,0:T(4,128)(2,1)S(1)}, u32[]{:S(2)}, u32[]{:S(2)}) %all-to-all-start.1) | async-done | bytes 1048608 | tf_op jit(solution)/shard_map/all_to_all | solution.py:151
  201.1 1.6 copy.34
  202.6 1.6 reshape_squeeze.3.basis_ref.coeff_ref
  204.2 9.4 %place.1 = bf16[1,512,4096]{2,1,0:T(8,128)(2,1)} custom-call(s32[256,4]{1,0:T(8,128)S(1)} %dynamic-slice_bitcast_fusion.rowmap_ref, s32[8,256,4]{2,1,0:T(8,128)S(1)} %bitcast.37, bf16[4,2,8,32,256]{4,3,2,1,0:T(8,128)(2,1)S(1)} %reshape_squeeze.3.basis_ref.coeff_ref, bf16[4,2,8,32,256]{4,3,2,1,0:T(8,128)(2,1)S(1)} %reshape_squeeze.3.basis_ref.coeff_ref, ...), custom_call_target="tpu_custom_call" | custom-call | tf_op jit(solution)/shard_map/place/pallas_call | solution.py:91
  (26 shorter events, 0.3 us)
Async XLA Ops:
  6.5 57.9 %copy-start = (bf16[1,256,2048]{2,1,0:T(8,128)(2,1)S(1)}, bf16[1,256,2048]{2,1,0:T(8,128)(2,1)}, u32[]{:S(2)}) copy-start(bf16[1,256,2048]{2,1,0:T(8,128)(2,1)} %param.8) | copy-start | bytes 3145732
  6.5 57.9 %all-gather.3.cloned.1.call-start = ((), (), s32[]{:S(2)}) async-start(), calls=%async_computation.2 | async-start | bytes 9437184 | tf_op jit(solution)/shard_map/all_gather | solution.py:130
  7.3 63.9 %copy-start.3 = (s32[32]{0:T(128)S(1)}, s32[32]{0:T(128)}, u32[]{:S(2)}) copy-start(s32[32]{0:T(128)} %param.14) | copy-start | bytes 388
  7.3 116.4 %copy-start.4 = (f32[1,256,2048]{2,1,0:T(8,128)S(1)}, f32[1,256,2048]{2,1,0:T(8,128)}, u32[]{:S(2)}) copy-start(f32[1,256,2048]{2,1,0:T(8,128)} %param.11) | copy-start | bytes 6291460
  7.3 116.4 %copy-start.5 = (f32[1,2048]{1,0:T(1,128)S(1)}, f32[1,2048]{1,0:T(1,128)}, u32[]{:S(2)}) copy-start(f32[1,2048]{1,0:T(1,128)} %param.10) | copy-start | bytes 24580
  7.3 116.4 %all-gather.5.cloned.1.call-start = ((), (), s32[]{:S(2)}) async-start(), calls=%async_computation.3 | async-start | bytes 9437184 | tf_op jit(solution)/shard_map/all_gather | solution.py:135
  123.7 6.2 %copy-start.1 = (f32[1,1,8,32,256]{4,3,2,1,0:T(8,128)S(1)}, f32[1,1,8,32,256]{4,3,2,1,0:T(8,128)}, u32[]{:S(2)}) copy-start(f32[1,1,8,32,256]{4,3,2,1,0:T(8,128)} %param.12) | copy-start | bytes 786436
  142.3 21.8 %all-to-all-start = ((bf16[32,2,2048]{2,1,0:T(2,128)(2,1)}), bf16[32,2,2048]{2,1,0:T(2,128)(2,1)S(1)}, u32[]{:S(2)}, u32[]{:S(2)}) async-start(bf16[32,2,2048]{2,1,0:T(2,128)(2,1)} %reshape.152), calls=%async_computation | async-start | bytes 524288 | tf_op jit(solution)/shard_map/all_to_all | solution.py:146
  166.3 7.7 %copy-start.2 = (s32[32,2048]{1,0:T(8,128)S(1)}, s32[32,2048]{1,0:T(8,128)}, u32[]{:S(2)}) copy-start(s32[32,2048]{1,0:T(8,128)} %param.13) | copy-start | bytes 786436
  168.0 33.0 %all-to-all-start.1 = ((bf16[32,4,4096]{2,1,0:T(4,128)(2,1)}), bf16[32,4,4096]{2,1,0:T(4,128)(2,1)S(1)}, u32[]{:S(2)}, u32[]{:S(2)}) async-start(bf16[32,4,4096]{2,1,0:T(4,128)(2,1)} %select_select_fusion), calls=%async_computation.1 | async-start | bytes 2097152 | tf_op jit(solution)/shard_map/all_to_all | solution.py:151
Sparse Core Ops, SparseCore 0:
  9.2 55.1 all-gather.2
  71.2 52.4 all-gather.4
where the time goes:
time: 221 us; the launch traced here: 220 us
  waiting for transfers between devices  147 us (67%)
  Pallas kernels  18 us (8%)
  starting transfers between devices  15.8 us (7%)
  between operations  13.6 us (6%)
  matrix products  12.8 us (6%)
  local copies, waits for them, and re-layouts  8.57 us (4%)
  other arithmetic  4.61 us (2%)
    all_gather x1, waiting for transfers between devices, body(): lax.all_gather(pivot_inverse, 'panel', axis=1, tiled=True)[0]  57.1 us
    all_gather x1, waiting for transfers between devices, body(): gathered = lax.all_gather(factor, 'panel', axis=0, tiled=True)  51.8 us
    all_to_all x1, waiting for transfers between devices, body(): lax.all_to_all(outgoing, 'front', split_axis=0, concat_axis=2, tiled=True)  26 us
    all_to_all x1, waiting for transfers between devices, body(): lax.all_to_all(packed, 'front', split_axis=0, concat_axis=0, tiled=True)  11.4 us
    all_to_all x1, starting transfers between devices, body(): lax.all_to_all(packed, 'front', split_axis=0, concat_axis=0, tiled=True)  10.1 us
    pallas_call x1, Pallas kernels, place(): pl.pallas_call(place_kernel, grid=(tiles,), in_specs=[pl.BlockSpec((tile,...  9.4 us
    pallas_call x1, Pallas kernels, compress(): pl.pallas_call(compress_kernel, out_shape=(out, out), name='compress', co...  8.6 us
    dot_general x1, matrix products, body(): jnp.dot(rows_here, lax.all_gather(pivot_inverse, 'panel', axis=1, tiled=T...  6.68 us
  transfers between devices with their start and end apart: 4, of which 4 were waited for; matrix products, arithmetic and copies ran while one was open for 1% of the time, Pallas kernels for 0%

commit v1 on v0

--- a/solution.py
+++ b/solution.py
@@ -9,6 +9,7 @@
 
 MAXKIDS = 4
 HI = lax.Precision.HIGHEST
+MESH = pl.DeviceIdType.MESH
 
 
 def dot(a, b, dims, precision=None):
@@ -17,7 +18,198 @@
     )
 
 
-def compress_kernel(schur_ref, omega_ref, basis_ref, coeff_ref):
+def factor_kernel(steps, coupling_hbm, inverse_ref, pivots_ref, trailing_hbm, schur_ref,
+                  coupling_ref, inverses, factors, scaled_ref, send_sem, recv_sem, local_sem):
+    panel = lax.axis_index("panel")
+    chip = panel // 2
+    core = panel % 2
+    other = 1 - core
+    up = (chip + 1) % 4
+    down = (chip + 3) % 4
+    far = (chip + 2) % 4
+    rows, cols = inverse_ref.shape
+    half = rows // 2
+    chunk = cols // steps
+    partner = chip * 2 + other
+    above = up * 2 + core
+    below = down * 2 + core
+
+    fetch_c = pltpu.make_async_copy(coupling_hbm, coupling_ref, local_sem.at[0])
+    fetch_t = pltpu.make_async_copy(trailing_hbm, schur_ref, local_sem.at[1])
+    fetch_w = pltpu.make_async_copy(inverse_ref, inverses.at[panel], local_sem.at[2])
+    fetch_w.start()
+    fetch_c.start()
+    fetch_t.start()
+
+    barrier = pltpu.get_barrier_semaphore()
+    for target in (partner, above, below):
+        pl.semaphore_signal(barrier, inc=1, device_id={"panel": target}, device_id_type=MESH)
+    pl.semaphore_wait(barrier, 3)
+
+    def view(phase, slot, part, c):
+        buffer = factors if phase else inverses
+        lanes = pl.ds(pl.multiple_of(c * chunk, chunk), chunk)
+        if part == 0:
+            return buffer.at[slot, :, lanes]
+        return buffer.at[slot, pl.ds((part - 1) * half, half), lanes]
+
+    mine = panel
+    low = down * 2 + core
+    high = up * 2 + core
+    table = (
+        (mine, 0, partner, partner),
+        (mine, 0, above, low),
+        (mine, 0, below, high),
+        (low, 0, partner, down * 2 + other),
+        (high, 0, partner, up * 2 + other),
+        (low, 1, above, far * 2 + core),
+        (high, 2, below, far * 2 + core),
+        (far * 2 + core, 1, partner, far * 2 + other),
+        (far * 2 + core, 2, partner, far * 2 + other),
+    )
+
+    def copy(phase, kind, c, source=None):
+        slot, part, target, _ = table[kind]
+        ref = view(phase, slot, part, c)
+        return pltpu.make_async_remote_copy(
+            src_ref=ref if source is None else source,
+            dst_ref=ref,
+            send_sem=send_sem.at[phase, c, kind],
+            recv_sem=recv_sem.at[phase, c, kind],
+            device_id={"panel": target},
+            device_id_type=MESH,
+        )
+
+    def arrived(phase, kind, c):
+        _, part, target, slot = table[kind]
+        ref = view(phase, slot, part, c)
+        pltpu.make_async_remote_copy(
+            src_ref=ref,
+            dst_ref=ref,
+            send_sem=send_sem.at[phase, c, kind],
+            recv_sem=recv_sem.at[phase, c, kind],
+            device_id={"panel": target},
+            device_id_type=MESH,
+        ).wait_recv()
+
+    def lanes_of(c):
+        return pl.ds(pl.multiple_of(c * chunk, chunk), chunk)
+
+    def send_inverse(c, carry):
+        for kind in (1, 2, 0):
+            copy(0, kind, c, inverse_ref.at[:, lanes_of(c)]).start()
+        return carry
+
+    def relay(phase, c):
+        arrived(phase, 1, c)
+        copy(phase, 5, c).start()
+        copy(phase, 3, c).start()
+        arrived(phase, 2, c)
+        copy(phase, 6, c).start()
+        copy(phase, 4, c).start()
+
+    def relay_far(phase, c):
+        arrived(phase, 5, c)
+        copy(phase, 7, c).start()
+        arrived(phase, 6, c)
+        copy(phase, 8, c).start()
+
+    def near_inverse(c, carry):
+        relay(0, c)
+        return carry
+
+    def make_factor(c, carry):
+        relay_far(0, c)
+        for kind in (0, 3, 4, 7, 8):
+            arrived(0, kind, c)
+        lanes = lanes_of(c)
+        total = dot(coupling_ref[:, :rows], inverses[0, :, lanes], ((1,), (0,)))
+        for q in range(1, cols // rows):
+            total = total + dot(
+                coupling_ref[:, q * rows:(q + 1) * rows], inverses[q, :, lanes], ((1,), (0,))
+            )
+        factor = total.astype(jnp.bfloat16)
+        factors[mine, :, lanes] = factor
+        scaled_ref[:, lanes] = (factor.astype(jnp.float32) / pivots_ref[:, lanes]).astype(jnp.bfloat16)
+        for kind in (1, 2, 0):
+            copy(1, kind, c).start()
+        return carry
+
+    def apply(slot, c):
+        lanes = lanes_of(c)
+        out = pl.ds(pl.multiple_of(slot * rows, rows), rows)
+        schur_ref[:, out] -= dot(scaled_ref[:, lanes], factors[slot, :, lanes], ((1,), (1,)))
+
+    def near_factor(c, carry):
+        apply(mine, c)
+        arrived(1, 0, c)
+        apply(partner, c)
+        relay(1, c)
+        apply(low, c)
+        apply(high, c)
+        arrived(1, 3, c)
+        apply(down * 2 + other, c)
+        arrived(1, 4, c)
+        apply(up * 2 + other, c)
+        return carry
+
+    def far_factor(c, carry):
+        relay_far(1, c)
+        apply(far * 2 + core, c)
+        arrived(1, 7, c)
+        arrived(1, 8, c)
+        apply(far * 2 + other, c)
+        return carry
+
+    lax.fori_loop(0, steps, send_inverse, 0)
+    fetch_w.wait()
+    fetch_c.wait()
+    lax.fori_loop(0, steps, near_inverse, 0)
+    lax.fori_loop(0, steps, make_factor, 0)
+    fetch_t.wait()
+    lax.fori_loop(0, steps, near_factor, 0)
+    lax.fori_loop(0, steps, far_factor, 0)
+
+    def drain(c, carry):
+        for phase in range(2):
+            for kind in range(9):
+                copy(phase, kind, c).wait_send()
+        return carry
+
+    lax.fori_loop(0, steps, drain, 0)
+
+
+def update(coupling, pivot_inverse, pivots, trailing):
+    rows, cols = coupling.shape
+    pieces = cols // rows
+    steps = 4
+    return pl.pallas_call(
+        functools.partial(factor_kernel, steps),
+        in_specs=[
+            pl.BlockSpec(memory_space=pltpu.HBM),
+            pl.BlockSpec(memory_space=pltpu.VMEM),
+            pl.BlockSpec(memory_space=pltpu.VMEM),
+            pl.BlockSpec(memory_space=pltpu.HBM),
+        ],
+        out_specs=pl.BlockSpec(memory_space=pltpu.VMEM),
+        out_shape=jax.ShapeDtypeStruct(trailing.shape, trailing.dtype),
+        scratch_shapes=[
+            pltpu.VMEM((rows, cols), jnp.bfloat16),
+            pltpu.VMEM((pieces, rows, cols), jnp.bfloat16),
+            pltpu.VMEM((pieces, rows, cols), jnp.bfloat16),
+            pltpu.VMEM((rows, cols), jnp.bfloat16),
+            pltpu.SemaphoreType.DMA((2, steps, 9)),
+            pltpu.SemaphoreType.DMA((2, steps, 9)),
+            pltpu.SemaphoreType.DMA((3,)),
+        ],
+        name="update",
+        compiler_params=pltpu.CompilerParams(
+            collective_id=0, has_side_effects=True, vmem_limit_bytes=60 * 1024 * 1024
+        ),
+    )(coupling, pivot_inverse, pivots, trailing)
+
+
+def compress_kernel(schur_ref, omega_ref, packed_ref):
     tiles, rank, tile = omega_ref.shape
     ys = []
     state = []
@@ -41,23 +233,209 @@
         inverse = a[j, :, rank:] * (1.0 / jnp.sqrt(diag))
         basis = dot(inverse, ys[j], ((1,), (0,)), HI)
         block = schur_ref[:, j * tile:(j + 1) * tile]
-        basis_ref[j] = basis.astype(jnp.bfloat16)
-        coeff_ref[j] = dot(basis, block, ((1,), (0,)), HI).astype(jnp.bfloat16)
+        packed_ref[j, :rank, :] = basis.astype(jnp.bfloat16)
+        packed_ref[j, rank:, :] = dot(basis, block, ((1,), (0,)), HI).astype(jnp.bfloat16)
 
 
 def compress(schur, omega):
     tiles, rank, tile = omega.shape
-    out = jax.ShapeDtypeStruct((tiles, rank, tile), jnp.bfloat16)
+    out = jax.ShapeDtypeStruct((tiles, 2 * rank, tile), jnp.bfloat16)
     return pl.pallas_call(
         compress_kernel,
-        out_shape=(out, out),
+        out_shape=out,
         name="compress",
         compiler_params=pltpu.CompilerParams(vmem_limit_bytes=48 * 1024 * 1024),
     )(schur, omega)
 
 
+class Exchange:
+    def __init__(self, picks, packed, ring, staged, kids, sems):
+        self.picks, self.packed, self.ring, self.staged, self.kids = picks, packed, ring, staged, kids
+        self.split_send, self.split_recv, self.ring_send, self.ring_recv, self.pick_send, self.pick_recv, self.own = sems
+        front = lax.axis_index("front")
+        self.z = front // 4
+        self.x = front % 4
+        chip = lax.axis_index("panel") // 2
+        self.tiles = [pl.ds(pl.multiple_of(2 * ((chip + d) % 4), 2), 2) for d in (0, 3, 1, 2)]
+
+    def across(self, step):
+        return self.z * 4 + (self.x + step) % 4
+
+    def greeted(self):
+        z = self.z
+        return [self.across(s) for s in (1, 2, 3)] + [
+            ((z + 1) % 8) * 4 + self.x, ((z + 7) % 8) * 4 + self.x]
+
+    def part(self, x):
+        return pl.ds(pl.multiple_of(16 * x, 16), 16)
+
+    def split(self, g, step):
+        return pltpu.make_async_remote_copy(
+            src_ref=self.packed.at[self.tiles[g], self.part((self.x + step) % 4), :],
+            dst_ref=self.ring[g].at[self.z, self.x],
+            send_sem=self.split_send.at[g, step - 1],
+            recv_sem=self.split_recv.at[g, step - 1],
+            device_id={"front": self.across(step)},
+            device_id_type=MESH,
+        )
+
+    def split_own(self, g):
+        return pltpu.make_async_copy(
+            self.packed.at[self.tiles[g], self.part(self.x), :],
+            self.ring[g].at[self.z, self.x],
+            self.own.at[g],
+        )
+
+    def split_start(self, g):
+        for step in (2, 1, 3):
+            self.split(g, step).start()
+        self.split_own(g).start()
+
+    def split_wait(self, g):
+        self.split_own(g).wait()
+        for step in (1, 3, 2):
+            ref = self.ring[g].at[self.z, (self.x + 4 - step) % 4]
+            pltpu.make_async_remote_copy(
+                src_ref=ref,
+                dst_ref=ref,
+                send_sem=self.split_send.at[g, step - 1],
+                recv_sem=self.split_recv.at[g, step - 1],
+                device_id={"front": self.across(step)},
+                device_id_type=MESH,
+            ).wait_recv()
+
+    def hop(self, g, way, k, incoming):
+        sign = -1 if way == 0 else 1
+        at = (self.z + 8 + sign * (k + incoming)) % 8
+        ref = self.ring[g].at[at]
+        if k == 3:
+            ref = self.ring[g].at[at, pl.ds(2 * way, 2)]
+        target = ((self.z + (1 if way == 0 else 7)) % 8) * 4 + self.x
+        return pltpu.make_async_remote_copy(
+            src_ref=ref,
+            dst_ref=ref,
+            send_sem=self.ring_send.at[g, way, k],
+            recv_sem=self.ring_recv.at[g, way, k],
+            device_id={"front": target},
+            device_id_type=MESH,
+        )
+
+    def ring_start(self, g):
+        self.split_wait(g)
+        for way in (0, 1):
+            self.hop(g, way, 0, 0).start()
+
+    def ring_step(self, g, k):
+        for way in (0, 1):
+            self.hop(g, way, k - 1, 1).wait_recv()
+            self.hop(g, way, k, 0).start()
+
+    def ring_end(self, g):
+        for way in (0, 1):
+            self.hop(g, way, 3, 1).wait_recv()
+
+    def pick(self, g, step):
+        return pltpu.make_async_remote_copy(
+            src_ref=self.staged.at[g, step - 1],
+            dst_ref=self.kids.at[:, self.tiles[g], self.part(self.x), :],
+            send_sem=self.pick_send.at[g, step - 1],
+            recv_sem=self.pick_recv.at[g, step - 1],
+            device_id={"front": self.across(step)},
+            device_id_type=MESH,
+        )
+
+    def pick_start(self, g):
+        for step in (2, 1, 3, 0):
+            parent = self.across(step)
+            for s in range(MAXKIDS):
+                child = self.picks[parent, s]
+                block = self.ring[g][child // 4, child % 4]
+                if step:
+                    self.staged[g, step - 1, s] = block
+                else:
+                    self.kids[s, self.tiles[g], self.part(self.x), :] = block
+            if step:
+                self.pick(g, step).start()
+
+    def pick_wait(self, g):
+        for step in (1, 3, 2):
+            ref = self.kids.at[:, self.tiles[g], self.part((self.x + 4 - step) % 4), :]
+            pltpu.make_async_remote_copy(
+                src_ref=ref,
+                dst_ref=ref,
+                send_sem=self.pick_send.at[g, step - 1],
+                recv_sem=self.pick_recv.at[g, step - 1],
+                device_id={"front": self.across(step)},
+                device_id_type=MESH,
+            ).wait_recv()
+
+    def drain(self, g):
+        for step in (1, 2, 3):
+            self.split(g, step).wait_send()
+            self.pick(g, step).wait_send()
+        for way in (0, 1):
+            for k in range(4):
+                self.hop(g, way, k, 0).wait_send()
+
+
+def exchange_scratch():
+    block = (2, 16, 256)
+    return [
+        pltpu.VMEM((4, 3, MAXKIDS) + block, jnp.bfloat16),
+    ] + [pltpu.VMEM((8, 4) + block, jnp.bfloat16)] * 4 + [pltpu.SemaphoreType.DMA(shape) for shape in (
+        (4, 3), (4, 3), (4, 2, 4), (4, 2, 4), (4, 3), (4, 3), (4,))]
+
+
+def exchange_kernel(picks, packed, kids, staged, *rest):
+    ex = Exchange(picks, packed, rest[:4], staged, kids, rest[4:])
+    barrier = pltpu.get_barrier_semaphore()
+    for target in ex.greeted():
+        pl.semaphore_signal(barrier, inc=1, device_id={"front": target}, device_id_type=MESH)
+    pl.semaphore_wait(barrier, 5)
+    for g in range(4):
+        ex.split_start(g)
+    for g in (0, 1):
+        ex.ring_start(g)
+    for k in (1, 2, 3):
+        for g in (0, 1):
+            ex.ring_step(g, k)
+    for g in (2, 3):
+        ex.ring_start(g)
+    for g in (0, 1):
+        ex.ring_end(g)
+        ex.pick_start(g)
+    for k in (1, 2, 3):
+        for g in (2, 3):
+            ex.ring_step(g, k)
+    for g in (2, 3):
+        ex.ring_end(g)
+        ex.pick_start(g)
+    for g in range(4):
+        ex.pick_wait(g)
+    for g in range(4):
+        ex.drain(g)
+
+
+def exchange(picks, packed):
+    tiles, depth, tile = packed.shape
+    return pl.pallas_call(
+        exchange_kernel,
+        in_specs=[
+            pl.BlockSpec(memory_space=pltpu.SMEM),
+            pl.BlockSpec(memory_space=pltpu.VMEM),
+        ],
+        out_specs=pl.BlockSpec(memory_space=pltpu.VMEM),
+        out_shape=jax.ShapeDtypeStruct((MAXKIDS, tiles, depth, tile), packed.dtype),
+        scratch_shapes=exchange_scratch(),
+        name="exchange",
+        compiler_params=pltpu.CompilerParams(
+            collective_id=1, has_side_effects=True, vmem_limit_bytes=48 * 1024 * 1024
+        ),
+    )(picks, packed)
+
+
 def place_kernel(rowmap_ref, colmap_ref, basis_ref, coeff_ref, base_ref, out_ref, rt_ref):
-    kids, _, tiles, rank, tile = basis_ref.shape
+    kids, tiles, rank, tile = basis_ref.shape
     height = out_ref.shape[1]
     width = out_ref.shape[2]
     j = pl.program_id(0)
@@ -69,14 +447,14 @@
         for s in range(kids):
             hot = jnp.where(rowmap_ref[:, s:s + 1] == high, 1.0, 0.0).astype(jnp.bfloat16)
             rt_ref[s] = dot(
-                basis_ref[s, 0].reshape(tiles * rank, tile), hot, ((1,), (0,))
+                basis_ref[s].reshape(tiles * rank, tile), hot, ((1,), (0,))
             ).astype(jnp.bfloat16)
 
     left = []
     right = []
     for s in range(kids):
         hot = jnp.where(colmap_ref[0, :, s:s + 1] == lanes, 1.0, 0.0).astype(jnp.bfloat16)
-        right.append(dot(coeff_ref[s, 0, 0], hot, ((1,), (0,))).astype(jnp.bfloat16))
+        right.append(dot(coeff_ref[s, 0], hot, ((1,), (0,))).astype(jnp.bfloat16))
         left.append(rt_ref[s, pl.ds(j * rank, rank), :])
     left = jnp.concatenate(left, axis=0)
     right = jnp.concatenate(right, axis=0)
@@ -85,7 +463,8 @@
 
 
 def place(rowmap, colmap, data, base):
-    kids, _, tiles, rank, tile = data.shape
+    kids, tiles, depth, tile = data.shape
+    rank = depth // 2
     _, height, total = base.shape
     width = total // tiles
     return pl.pallas_call(
@@ -94,8 +473,8 @@
         in_specs=[
             pl.BlockSpec((tile, kids), lambda j: (0, 0)),
             pl.BlockSpec((1, tile, kids), lambda j: (j, 0, 0)),
-            pl.BlockSpec((kids, 1, tiles, rank, tile), lambda j: (0, 0, 0, 0, 0)),
-            pl.BlockSpec((kids, 1, 1, rank, tile), lambda j: (0, 1, j, 0, 0)),
+            pl.BlockSpec((kids, tiles, rank, tile), lambda j: (0, 0, 0, 0)),
+            pl.BlockSpec((kids, 1, rank, tile), lambda j: (0, j, 1, 0)),
             pl.BlockSpec((1, height, width), lambda j: (0, 0, j)),
         ],
         out_specs=pl.BlockSpec((1, height, width), lambda j: (0, 0, j)),
@@ -123,33 +502,15 @@
 
 
 def body(coupling, pivot_inverse, pivots, trailing, sketch, extend_map, parent_of, parent_base):
-    rows_here = coupling[0]
-    row_dev = rows_here.shape[0]
-    factor_sum = jnp.dot(
-        rows_here,
-        lax.all_gather(pivot_inverse, "panel", axis=1, tiled=True)[0],
-        preferred_element_type=jnp.float32,
-    )
-    factor = factor_sum.astype(jnp.bfloat16)
-    scaled = (factor.astype(jnp.float32) / pivots[0][None, :]).astype(jnp.bfloat16)
-    gathered = lax.all_gather(factor, "panel", axis=0, tiled=True)
-    update = dot(scaled, gathered, ((1,), (1,)))
-    schur = trailing[0] - update
-    basis, coeff = compress(schur, sketch[0, 0])
+    row_dev = coupling.shape[1]
+    schur = update(coupling[0], pivot_inverse[0], pivots, trailing[0])
+    packed = compress(schur, sketch[0, 0])
 
     panels = lax.axis_size("panel")
     owner = lax.axis_index("front")
     panel_here = lax.axis_index("panel")
-    fronts = parent_of.shape[0]
     children, present = family(parent_of)
-    packed = jnp.stack((basis, coeff)).reshape(fronts, -1)
-    spread = lax.all_to_all(packed, "front", split_axis=0, concat_axis=0, tiled=True)
-    chosen = jnp.take(spread, children.reshape(-1), axis=0)
-    outgoing = jnp.where(present.reshape(-1)[:, None], chosen, jnp.zeros((), jnp.bfloat16)).reshape(
-        fronts, MAXKIDS, -1
-    )
-    received = lax.all_to_all(outgoing, "front", split_axis=0, concat_axis=2, tiled=True)
-    data = received[0].reshape((MAXKIDS, 2) + basis.shape)
+    data = exchange(children, packed)
     maps = jnp.where(present[owner][:, None], extend_map[children[owner]], -1)
     colmap = jnp.transpose(maps).reshape(panels, row_dev, MAXKIDS)
     rowmap = lax.dynamic_index_in_dim(colmap, panel_here, 0, keepdims=False)

time: 221 us -> 147 us (0.67)
  waiting for transfers between devices: 147 us -> 0 us
  Pallas kernels: 18 us -> 141 us
  starting transfers between devices: 15.8 us -> 0 us
  between operations: 13.6 us -> 0.07 us
  matrix products: 12.8 us -> 0 us
  local copies, waits for them, and re-layouts: 8.57 us -> 3 us
  other arithmetic: 4.61 us -> 1.98 us
    pallas_call x1 -> x3, Pallas kernels: 8.6 us -> 131 us  [the longest x1 77.3 us: update(): pl.pallas_call(functools.partial(factor_kernel, steps), in_specs=[pl.Bloc...]
    all_gather x2 -> x0, waiting for transfers between devices: 109 us -> none  [the longest x1 57.1 us: body(): lax.all_gather(pivot_inverse, 'panel', axis=1, tiled=True)[0]]
    all_to_all x2 -> x0, waiting for transfers between devices: 37.4 us -> none  [the longest x1 26 us: body(): lax.all_to_all(outgoing, 'front', split_axis=0, concat_axis=2, tiled=True)]
    all_to_all x2 -> x0, starting transfers between devices: 15.7 us -> none  [the longest x1 10.1 us: body(): lax.all_to_all(packed, 'front', split_axis=0, concat_axis=0, tiled=True)]
    dot_general x2 -> x0, matrix products: 12.8 us -> none  [the longest x1 6.68 us: body(): jnp.dot(rows_here, lax.all_gather(pivot_inverse, 'panel', axis=1, tiled=T...]
    all_to_all x1 -> x0, other arithmetic: 2.26 us -> none  [body(): lax.all_to_all(packed, 'front', split_axis=0, concat_axis=0, tiled=True)]
  transfers between devices with their start and end apart: 4 -> 0, of which waited for: 4 -> 0; matrix products, arithmetic and copies ran while one was open for 1% -> 0% of each run, Pallas kernels for 0% -> 0%
where the time goes in v1:
time: 147 us; the launch traced here: 146 us
  Pallas kernels  141 us (96%)
  local copies, waits for them, and re-layouts  3 us (2%)
  other arithmetic  1.98 us (1%)
    pallas_call x1, Pallas kernels, update(): pl.pallas_call(functools.partial(factor_kernel, steps), in_specs=[pl.Bloc...  77.3 us
    pallas_call x1, Pallas kernels, exchange(): pl.pallas_call(exchange_kernel, in_specs=[pl.BlockSpec(memory_space=pltpu...  45.5 us
    pallas_call x1, Pallas kernels, place(): pl.pallas_call(place_kernel, grid=(tiles,), in_specs=[pl.BlockSpec((tile,...  9.39 us
    pallas_call x1, Pallas kernels, compress(): pl.pallas_call(compress_kernel, out_shape=out, name='compress', compiler_...  8.6 us

profile of v1, /device:TPU:2, one launch (start us, length us, event | category | flops | bytes accessed | tf_op | source)
XLA Modules:
  0.0 145.8 jit_solution(3116500889088574867)
XLA Ops:
  0.0 0.0 copy-start
  0.0 0.0 copy-start.2
  0.0 0.9 select_reduce_fusion
  0.9 0.7 iota_compare_fusion.1
  1.6 0.2 and_reduce_fusion
  1.7 0.2 fusion
  1.9 0.2 dynamic-slice_reduce_fusion.1
  2.1 0.2 dynamic-slice_reduce_fusion
  2.3 0.1 copy.13.picks
  2.4 0.0 copy-done
  2.4 0.6 gather_fusion
  3.0 0.1 select_bitcast_fusion
  3.0 0.4 copy.12
  3.4 77.3 %update.1.schur_ref = f32[256,2048]{1,0:T(8,128)} custom-call(bf16[256,2048]{1,0:T(8,128)(2,1)} %bitcast.17, bf16[256,2048]{1,0:T(8,128)(2,1)} %bitcast.18, f32[1,2048]{1,0:T(1,128)} %pivots_ref.1, f32[256,2048]{1,0:T(8,128)} %bitcast.16), custom_call_target="tpu_custom_call" | custom-call | tf_op jit(solution)/shard_map/update/pallas_call | solution.py:186
  80.8 0.0 copy-done.2
  80.8 0.0 copy-start.1
  80.8 1.6 %copy-done.1 = f32[256,2048]{1,0:T(8,128)S(1)} copy-done((f32[256,2048]{1,0:T(8,128)S(1)}, f32[256,2048]{1,0:T(8,128)}, u32[]{:S(2)}) %copy-start.1) | copy-done | bytes 2097176
  82.4 8.6 %compress.1.packed = bf16[8,64,256]{2,1,0:T(8,128)(2,1)S(1)} custom-call(f32[256,2048]{1,0:T(8,128)S(1)} %copy-done.1, f32[8,32,256]{2,1,0:T(8,128)S(1)} %bitcast.15), custom_call_target="tpu_custom_call" | custom-call | tf_op jit(solution)/shard_map/compress/pallas_call | solution.py:243
  91.0 45.5 %exchange.1.basis_ref.coeff_ref = bf16[4,8,64,256]{3,2,1,0:T(8,128)(2,1)S(1)} custom-call(s32[32,4]{1,0:T(8,128)S(1)} %copy.13.picks, bf16[8,64,256]{2,1,0:T(8,128)(2,1)S(1)} %compress.1.packed), custom_call_target="tpu_custom_call" | custom-call | tf_op jit(solution)/shard_map/exchange/pallas_call | solution.py:421
  136.4 9.4 %place.1 = bf16[1,512,4096]{2,1,0:T(8,128)(2,1)} custom-call(s32[256,4]{1,0:T(8,128)S(1)} %dynamic-slice_bitcast_fusion.rowmap_ref, s32[8,256,4]{2,1,0:T(8,128)S(1)} %bitcast.14, bf16[4,8,64,256]{3,2,1,0:T(8,128)(2,1)S(1)} %exchange.1.basis_ref.coeff_ref, bf16[4,8,64,256]{3,2,1,0:T(8,128)(2,1)S(1)} %exchange.1.basis_ref.coeff_ref, bf16[1,512,4096]{2,1,0:T(8,128)(2,1)} %base_ref.1), custom_call_target="tpu_custom_call" | custom-call | tf_op jit(solution)/shard_map/place/pallas_call | solution.py:470
  (4 shorter events, 0.0 us)
Async XLA Ops:
  0.0 2.4 %copy-start = (s32[32,2048]{1,0:T(8,128)S(1)}, s32[32,2048]{1,0:T(8,128)}, u32[]{:S(2)}) copy-start(s32[32,2048]{1,0:T(8,128)} %param.13) | copy-start | bytes 786436
  0.0 80.8 %copy-start.2 = (f32[1,1,8,32,256]{4,3,2,1,0:T(8,128)S(1)}, f32[1,1,8,32,256]{4,3,2,1,0:T(8,128)}, u32[]{:S(2)}) copy-start(f32[1,1,8,32,256]{4,3,2,1,0:T(8,128)} %param.12) | copy-start | bytes 786436
  80.8 1.6 %copy-start.1 = (f32[256,2048]{1,0:T(8,128)S(1)}, f32[256,2048]{1,0:T(8,128)}, u32[]{:S(2)}) copy-start(f32[256,2048]{1,0:T(8,128)} %update.1.schur_ref) | copy-start | bytes 6291460

commit v2 on v1

v2 whole, which is shorter than its diff:
```python
import functools

import jax
import jax.numpy as jnp
from jax import lax
from jax.experimental import pallas as pl
from jax.experimental.pallas import tpu as pltpu
from jax.sharding import PartitionSpec as P

MAXKIDS = 4
HI = lax.Precision.HIGHEST
MESH = pl.DeviceIdType.MESH


def dot(a, b, dims, precision=None):
    return lax.dot_general(
        a, b, (dims, ((), ())), precision=precision, preferred_element_type=jnp.float32
    )


def level_kernel(steps, picks, counts, coupling_hbm, inverse_hbm, pivots_ref, trailing_hbm, omega_hbm, maps_hbm, tall_hbm, wide_hbm,
                 coupling_ref, inverses, factors, scaled_ref, schur_ref, omega_ref,
                 maps_ref, spots_ref, own_ref, send_sem, recv_sem, local_sem, staged, *rest):
    panel = lax.axis_index("panel")
    chip = panel // 2
    core = panel % 2
    other = 1 - core
    up = (chip + 1) % 4
    down = (chip + 3) % 4
    far = (chip + 2) % 4
    rows, cols = coupling_ref.shape
    half = rows // 2
    chunk = cols // steps
    partner = chip * 2 + other
    above = up * 2 + core
    below = down * 2 + core

    ring, packed, kids, tall, wide = (rest[4 * i:4 * i + 4] for i in range(5))
    fetch_w = pltpu.make_async_copy(inverse_hbm, own_ref, local_sem.at[0])
    fetch_v = pltpu.make_async_copy(inverse_hbm, inverses.at[panel], local_sem.at[13])
    fetch_c = pltpu.make_async_copy(coupling_hbm, coupling_ref, local_sem.at[1])
    fetch_t = pltpu.make_async_copy(trailing_hbm, schur_ref, local_sem.at[2])
    fetch_o = pltpu.make_async_copy(omega_hbm, omega_ref, local_sem.at[3])
    fetch_w.start()
    fetch_v.start()
    fetch_c.start()
    fetch_t.start()
    fetch_m = pltpu.make_async_copy(maps_hbm, maps_ref, local_sem.at[4])
    fetch_o.start()
    fetch_m.start()

    ex = Exchange(picks, packed, ring, staged, kids, rest[20:])
    barrier = pltpu.get_barrier_semaphore()
    for target in (partner, above, below):
        pl.semaphore_signal(barrier, inc=1, device_id={"panel": target}, device_id_type=MESH)
    for target in ex.greeted():
        pl.semaphore_signal(barrier, inc=1, device_id={"front": target}, device_id_type=MESH)
    pl.semaphore_wait(barrier, 8)

    def view(phase, slot, part, c):
        buffer = factors if phase else inverses
        lanes = pl.ds(pl.multiple_of(c * chunk, chunk), chunk)
        if part == 0:
            return buffer.at[slot, :, lanes]
        return buffer.at[slot, pl.ds((part - 1) * half, half), lanes]

    mine = panel
    low = down * 2 + core
    high = up * 2 + core
    table = (
        (mine, 0, partner, partner),
        (mine, 0, above, low),
        (mine, 0, below, high),
        (low, 0, partner, down * 2 + other),
        (high, 0, partner, up * 2 + other),
        (low, 1, above, far * 2 + core),
        (high, 2, below, far * 2 + core),
        (far * 2 + core, 1, partner, far * 2 + other),
        (far * 2 + core, 2, partner, far * 2 + other),
    )

    def copy(phase, kind, c, source=None):
        slot, part, target, _ = table[kind]
        ref = view(phase, slot, part, c)
        return pltpu.make_async_remote_copy(
            src_ref=ref if source is None else source,
            dst_ref=ref,
            send_sem=send_sem.at[phase, c, kind],
            recv_sem=recv_sem.at[phase, c, kind],
            device_id={"panel": target},
            device_id_type=MESH,
        )

    def arrived(phase, kind, c):
        _, part, target, slot = table[kind]
        ref = view(phase, slot, part, c)
        pltpu.make_async_remote_copy(
            src_ref=ref,
            dst_ref=ref,
            send_sem=send_sem.at[phase, c, kind],
            recv_sem=recv_sem.at[phase, c, kind],
            device_id={"panel": target},
            device_id_type=MESH,
        ).wait_recv()

    def lanes_of(c):
        return pl.ds(pl.multiple_of(c * chunk, chunk), chunk)

    def send_inverse(c, carry):
        for kind in (1, 2, 0):
            copy(0, kind, c, own_ref.at[:, lanes_of(c)]).start()
        return carry

    def relay(phase, c):
        arrived(phase, 1, c)
        copy(phase, 5, c).start()
        copy(phase, 3, c).start()
        arrived(phase, 2, c)
        copy(phase, 6, c).start()
        copy(phase, 4, c).start()

    def relay_far(phase, c):
        arrived(phase, 5, c)
        copy(phase, 7, c).start()
        arrived(phase, 6, c)
        copy(phase, 8, c).start()

    def near_inverse(c, carry):
        relay(0, c)
        return carry

    def make_factor(c, carry):
        relay_far(0, c)
        for kind in (0, 3, 4, 7, 8):
            arrived(0, kind, c)
        lanes = lanes_of(c)
        total = dot(coupling_ref[:, :rows], inverses[0, :, lanes], ((1,), (0,)))
        for q in range(1, cols // rows):
            total = total + dot(
                coupling_ref[:, q * rows:(q + 1) * rows], inverses[q, :, lanes], ((1,), (0,))
            )
        factor = total.astype(jnp.bfloat16)
        factors[mine, :, lanes] = factor
        scaled_ref[:, lanes] = (factor.astype(jnp.float32) / pivots_ref[:, lanes]).astype(jnp.bfloat16)
        for kind in (1, 2, 0):
            copy(1, kind, c).start()
        return carry

    def apply(slot, c):
        lanes = lanes_of(c)
        out = pl.ds(pl.multiple_of(slot * rows, rows), rows)
        schur_ref[:, out] -= dot(scaled_ref[:, lanes], factors[slot, :, lanes], ((1,), (1,)))

    def own_tiles(c, carry):
        apply(mine, c)
        arrived(1, 0, c)
        apply(partner, c)
        return carry

    def near_factor(c):
        relay(1, c)
        apply(low, c)
        apply(high, c)
        arrived(1, 3, c)
        apply(down * 2 + other, c)
        arrived(1, 4, c)
        apply(up * 2 + other, c)

    def far_factor(c):
        apply(far * 2 + core, c)
        arrived(1, 7, c)
        arrived(1, 8, c)
        apply(far * 2 + other, c)

    def squeeze(*groups, between=lambda: None):
        tiles = [2 * ((chip + (0, 3, 1, 2)[g]) % 4) + i for g in groups for i in range(2)]
        compress(schur_ref, omega_ref, [packed[g].at[i] for g in groups for i in range(2)], tiles, between)

    def first_hops():
        ex.ring_step(1, 1)
        ex.ring_step(2, 1)

    def spots(s, block, size):
        front = lax.axis_index("front")
        lanes = pl.ds(pl.multiple_of(block * rows, rows), rows)
        where = jnp.where(s < counts[front], maps_ref[pl.ds(picks[front, s], 1), lanes], -1)
        ids = lax.broadcasted_iota(jnp.int32, (size, rows), 0)
        return jnp.where(where == ids, 1.0, 0.0).astype(jnp.bfloat16)

    def row_spots():
        for s in range(MAXKIDS):
            spots_ref[s] = spots(s, panel, spots_ref.shape[1])

    def outward(g, which):
        ref, hbm = ((tall[g], tall_hbm), (wide[g], wide_hbm))[which]
        return pltpu.make_async_copy(ref, hbm.at[ex.tiles[g]], local_sem.at[5 + 2 * g + which])

    def scatter(g):
        ex.pick_wait(g)
        first = 2 * ((chip + (0, 3, 1, 2)[g]) % 4)
        rank = omega_ref.shape[1]
        for s in range(MAXKIDS):
            block = kids[g][s, :, :rank, :].reshape(2 * rank, rows)
            high = dot(block, spots_ref[s], ((1,), (1,))).astype(jnp.bfloat16)
            for i in range(2):
                tall[g][i, s * rank:(s + 1) * rank, :] = high[i * rank:(i + 1) * rank]
                coeff = kids[g][s, i, rank:, :]
                broad = dot(coeff, spots(s, first + i, wide[g].shape[2]), ((1,), (1,)))
                wide[g][i, s * rank:(s + 1) * rank, :] = broad.astype(jnp.bfloat16)
        for which in range(2):
            outward(g, which).start()

    fetch_w.wait()
    lax.fori_loop(0, steps, send_inverse, 0)
    fetch_m.wait()
    row_spots()
    fetch_c.wait()
    fetch_v.wait()
    lax.fori_loop(0, steps, near_inverse, 0)
    lax.fori_loop(0, steps, make_factor, 0)
    fetch_t.wait()
    fetch_o.wait()
    lax.fori_loop(0, steps, own_tiles, 0)
    squeeze(0)
    ex.split_start(0)
    near_factor(0)
    near_factor(1)
    ex.ring_start(0)
    near_factor(2)
    ex.ring_step(0, 1)
    near_factor(3)
    ex.ring_step(0, 2)
    squeeze(1, 2)
    ex.split_start(1)
    ex.split_start(2)
    ex.ring_step(0, 3)
    relay_far(1, 0)
    relay_far(1, 1)
    far_factor(0)
    far_factor(1)
    relay_far(1, 2)
    ex.ring_start(1)
    ex.ring_start(2)
    far_factor(2)
    relay_far(1, 3)
    ex.ring_end(0)
    ex.pick_start(0)
    far_factor(3)
    squeeze(3, between=first_hops)
    ex.split_start(3)
    ex.ring_start(3)
    ex.ring_step(1, 2)
    ex.ring_step(2, 2)
    ex.ring_step(3, 1)
    ex.ring_step(1, 3)
    ex.ring_step(2, 3)
    ex.ring_step(3, 2)
    for g in (1, 2):
        ex.ring_end(g)
        ex.pick_start(g)
    scatter(0)
    ex.ring_step(3, 3)
    scatter(1)
    scatter(2)
    ex.ring_end(3)
    ex.pick_start(3)
    scatter(3)
    for g in range(4):
        ex.drain(g)
        for which in range(2):
            outward(g, which).wait()

    def drain(c, carry):
        for phase in range(2):
            for kind in range(9):
                copy(phase, kind, c).wait_send()
        return carry

    lax.fori_loop(0, steps, drain, 0)


def level(picks, counts, coupling, pivot_inverse, pivots, trailing, omega, maps, height):
    rows, cols = coupling.shape
    tiles, rank, tile = omega.shape
    pieces = cols // rows
    steps = 4
    hbm = pl.BlockSpec(memory_space=pltpu.HBM)
    vmem = pl.BlockSpec(memory_space=pltpu.VMEM)
    spread = (tiles, MAXKIDS * rank, height)
    return pl.pallas_call(
        functools.partial(level_kernel, steps),
        in_specs=[pl.BlockSpec(memory_space=pltpu.SMEM)] * 2 + [hbm, hbm, vmem, hbm, hbm, hbm],
        out_specs=(hbm, hbm),
        out_shape=(jax.ShapeDtypeStruct(spread, jnp.bfloat16),) * 2,
        scratch_shapes=[
            pltpu.VMEM((rows, cols), jnp.bfloat16),
            pltpu.VMEM((pieces, rows, cols), jnp.bfloat16),
            pltpu.VMEM((pieces, rows, cols), jnp.bfloat16),
            pltpu.VMEM((rows, cols), jnp.bfloat16),
            pltpu.VMEM((rows, cols), jnp.float32),
            pltpu.VMEM((tiles, rank, tile), jnp.float32),
            pltpu.VMEM(maps.shape, jnp.int32),
            pltpu.VMEM((MAXKIDS, height, tile), jnp.bfloat16),
            pltpu.VMEM((rows, cols), jnp.bfloat16),
            pltpu.SemaphoreType.DMA((2, steps, 9)),
            pltpu.SemaphoreType.DMA((2, steps, 9)),
            pltpu.SemaphoreType.DMA((14,)),
        ] + exchange_scratch(rank, tile, height),
        name="level",
        compiler_params=pltpu.CompilerParams(
            collective_id=0, has_side_effects=True, vmem_limit_bytes=60 * 1024 * 1024
        ),
    )(picks, counts, coupling, pivot_inverse, pivots, trailing, omega, maps)


def halves(value):
    high = value.astype(jnp.bfloat16)
    return high, (value - high.astype(jnp.float32)).astype(jnp.bfloat16)


def fine(a, b, dims):
    a_high, a_low = halves(a)
    b_high, b_low = halves(b)
    return dot(a_high, b_high, dims) + (dot(a_high, b_low, dims) + dot(a_low, b_high, dims))


def compress(schur_ref, omega_ref, packed, tiles, between):
    _, rank, tile = omega_ref.shape
    ys = []
    state = []
    row_id = lax.broadcasted_iota(jnp.int32, (rank, rank), 0)
    col_id = lax.broadcasted_iota(jnp.int32, (rank, rank), 1)
    eye = jnp.where(row_id == col_id, 1.0, 0.0).astype(jnp.float32)
    spans = [pl.ds(pl.multiple_of(j * tile, tile), tile) for j in tiles]
    for j, span in zip(tiles, spans):
        y = fine(omega_ref[j], schur_ref[:, span], ((1,), (1,)))
        ys.append(y)
        state.append(jnp.concatenate([dot(y, y, ((1,), (1,)), HI), eye], axis=1))
    a = jnp.stack(state)
    rows = lax.broadcasted_iota(jnp.int32, (len(tiles), rank, 1), 1)
    lane = (len(tiles), 1, a.shape[-1])
    first = jnp.broadcast_to(1.0 / a[:, :1, :1], lane)
    for k in range(0, rank, 2):
        col0 = jnp.broadcast_to(jnp.where(rows > k, a[:, :, k:k + 1], 0.0), a.shape)
        col1 = jnp.broadcast_to(jnp.where(rows > k + 1, a[:, :, k + 1:k + 2], 0.0), a.shape)
        cross = col0[:, k + 1:k + 2, :]
        ratio = cross * first
        second = 1.0 / (jnp.broadcast_to(a[:, k + 1:k + 2, k + 1:k + 2], lane) - ratio * cross)
        row0 = a[:, k:k + 1, :]
        row1 = a[:, k + 1:k + 2, :] - ratio * row0
        col1 = jnp.where(rows > k + 1, col1 - col0 * ratio, 0.0)
        scaled0 = row0 * first
        if k + 2 < rank:
            after = jnp.broadcast_to(a[:, k + 2:k + 3, k + 2:k + 3], lane)
            low0 = col0[:, k + 2:k + 3, :]
            low1 = col1[:, k + 2:k + 3, :]
            first = 1.0 / (after - low0 * low0 * first - low1 * low1 * second)
        a = a - col0 * scaled0 - col1 * (row1 * second)
    between()
    for i, (j, span) in enumerate(zip(tiles, spans)):
        diag = jnp.sum(jnp.where(row_id == col_id, a[i, :, :rank], 0.0), axis=1, keepdims=True)
        inverse = a[i, :, rank:] * (1.0 / jnp.sqrt(diag))
        basis = dot(inverse, ys[i], ((1,), (0,)), HI)
        packed[i][:rank, :] = basis.astype(jnp.bfloat16)
        packed[i][rank:, :] = fine(basis, schur_ref[:, span], ((1,), (0,))).astype(jnp.bfloat16)


class Exchange:
    def __init__(self, picks, packed, ring, staged, kids, sems):
        self.picks, self.packed, self.ring, self.staged, self.kids = picks, packed, ring, staged, kids
        self.split_send, self.split_recv, self.ring_send, self.ring_recv, self.pick_send, self.pick_recv, self.own = sems
        front = lax.axis_index("front")
        self.z = front // 4
        self.x = front % 4
        chip = lax.axis_index("panel") // 2
        self.tiles = [pl.ds(pl.multiple_of(2 * ((chip + d) % 4), 2), 2) for d in (0, 3, 1, 2)]

    def across(self, step):
        return self.z * 4 + (self.x + step) % 4

    def greeted(self):
        z = self.z
        return [self.across(s) for s in (1, 2, 3)] + [
            ((z + 1) % 8) * 4 + self.x, ((z + 7) % 8) * 4 + self.x]

    def part(self, x):
        return pl.ds(pl.multiple_of(16 * x, 16), 16)

    def split(self, g, step):
        return pltpu.make_async_remote_copy(
            src_ref=self.packed[g].at[:, self.part((self.x + step) % 4), :],
            dst_ref=self.ring[g].at[self.z, self.x],
            send_sem=self.split_send.at[g, step - 1],
            recv_sem=self.split_recv.at[g, step - 1],
            device_id={"front": self.across(step)},
            device_id_type=MESH,
        )

    def split_own(self, g):
        return pltpu.make_async_copy(
            self.packed[g].at[:, self.part(self.x), :],
            self.ring[g].at[self.z, self.x],
            self.own.at[g],
        )

    def split_start(self, g):
        for step in (2, 1, 3):
            self.split(g, step).start()
        self.split_own(g).start()

    def split_wait(self, g):
        self.split_own(g).wait()
        for step in (1, 3, 2):
            ref = self.ring[g].at[self.z, (self.x + 4 - step) % 4]
            pltpu.make_async_remote_copy(
                src_ref=ref,
                dst_ref=ref,
                send_sem=self.split_send.at[g, step - 1],
                recv_sem=self.split_recv.at[g, step - 1],
                device_id={"front": self.across(step)},
                device_id_type=MESH,
            ).wait_recv()

    def hop(self, g, way, k, incoming):
        sign = -1 if way == 0 else 1
        at = (self.z + 8 + sign * (k + incoming)) % 8
        ref = self.ring[g].at[at]
        if k == 3:
            ref = self.ring[g].at[at, pl.ds(2 * way, 2)]
        target = ((self.z + (1 if way == 0 else 7)) % 8) * 4 + self.x
        return pltpu.make_async_remote_copy(
            src_ref=ref,
            dst_ref=ref,
            send_sem=self.ring_send.at[g, way, k],
            recv_sem=self.ring_recv.at[g, way, k],
            device_id={"front": target},
            device_id_type=MESH,
        )

    def ring_start(self, g):
        self.split_wait(g)
        for way in (0, 1):
            self.hop(g, way, 0, 0).start()

    def ring_step(self, g, k):
        for way in (0, 1):
            self.hop(g, way, k - 1, 1).wait_recv()
            self.hop(g, way, k, 0).start()

    def ring_end(self, g):
        for way in (0, 1):
            self.hop(g, way, 3, 1).wait_recv()

    def pick(self, g, step):
        return pltpu.make_async_remote_copy(
            src_ref=self.staged.at[g, step - 1],
            dst_ref=self.kids[g].at[:, :, self.part(self.x), :],
            send_sem=self.pick_send.at[g, step - 1],
            recv_sem=self.pick_recv.at[g, step - 1],
            device_id={"front": self.across(step)},
            device_id_type=MESH,
        )

    def pick_start(self, g):
        for step in (2, 1, 3, 0):
            for s in range(MAXKIDS):
                child = self.picks[self.across(step), s]
                block = self.ring[g][child // 4, child % 4]
                if step:
                    self.staged[g, step - 1, s] = block
                else:
                    self.kids[g][s, :, self.part(self.x), :] = block
        for step in (2, 1, 3):
            self.pick(g, step).start()

    def pick_wait(self, g):
        for step in (1, 3, 2):
            ref = self.kids[g].at[:, :, self.part((self.x + 4 - step) % 4), :]
            pltpu.make_async_remote_copy(
                src_ref=ref,
                dst_ref=ref,
                send_sem=self.pick_send.at[g, step - 1],
                recv_sem=self.pick_recv.at[g, step - 1],
                device_id={"front": self.across(step)},
                device_id_type=MESH,
            ).wait_recv()

    def drain(self, g):
        for step in (1, 2, 3):
            self.split(g, step).wait_send()
            self.pick(g, step).wait_send()
        for way in (0, 1):
            for k in range(4):
                self.hop(g, way, k, 0).wait_send()


def exchange_scratch(rank, tile, height):
    block = (2, 16, tile)
    shapes = [(8, 4) + block, (2, 2 * rank, tile), (MAXKIDS, 2, 2 * rank, tile)] + [(2, MAXKIDS * rank, height)] * 2
    return [pltpu.VMEM((4, 3, MAXKIDS) + block, jnp.bfloat16)] + [
        pltpu.VMEM(shape, jnp.bfloat16) for shape in shapes for _ in range(4)
    ] + [pltpu.SemaphoreType.DMA(shape) for shape in (
        (4, 3), (4, 3), (4, 2, 4), (4, 2, 4), (4, 3), (4, 3), (4,))]


def place_kernel(parts, tall_hbm, wide_hbm, base_hbm, out_hbm, tall_ref, wide_ref, base_ref, out_ref, sems):
    tiles = tall_ref.shape[0]
    width = wide_ref.shape[2]
    each = tiles // parts
    fetches = []
    for p in range(parts):
        some = pl.ds(p * each, each)
        lanes = pl.ds(p * each * width, each * width)
        fetches.append([
            pltpu.make_async_copy(tall_hbm.at[some], tall_ref.at[some], sems.at[0, p]),
            pltpu.make_async_copy(wide_hbm.at[some], wide_ref.at[some], sems.at[1, p]),
            pltpu.make_async_copy(base_hbm.at[:, lanes], base_ref.at[:, lanes], sems.at[2, p]),
        ])
        for fetch in fetches[p]:
            fetch.start()
    stores = []
    for p in range(parts):
        for fetch in fetches[p]:
            fetch.wait()
        for j in range(p * each, (p + 1) * each):
            lanes = slice(j * width, (j + 1) * width)
            total = dot(tall_ref[j], wide_ref[j], ((0,), (0,)))
            out_ref[:, lanes] = (base_ref[:, lanes].astype(jnp.float32) + total).astype(jnp.bfloat16)
        lanes = pl.ds(p * each * width, each * width)
        store = pltpu.make_async_copy(out_ref.at[:, lanes], out_hbm.at[:, lanes], sems.at[3, p])
        store.start()
        stores.append(store)
    for store in stores:
        store.wait()


def place(tall, wide, base):
    hbm = pl.BlockSpec(memory_space=pltpu.HBM)
    parts = 4
    return pl.pallas_call(
        functools.partial(place_kernel, parts),
        in_specs=[hbm] * 3,
        out_specs=hbm,
        out_shape=jax.ShapeDtypeStruct(base.shape, base.dtype),
        scratch_shapes=[pltpu.VMEM(a.shape, a.dtype) for a in (tall, wide, base, base)]
        + [pltpu.SemaphoreType.DMA((4, parts))],
        name="place",
        compiler_params=pltpu.CompilerParams(vmem_limit_bytes=60 * 1024 * 1024),
    )(tall, wide, base)


def family(parent_of):
    ids = jnp.arange(parent_of.shape[0], dtype=jnp.int32)
    earlier = (parent_of[:, None] == parent_of[None, :]) & (ids[None, :] < ids[:, None])
    position = jnp.sum(earlier.astype(jnp.int32), axis=1)
    takes = parent_of[None, :] == ids[:, None]
    slots = jnp.arange(MAXKIDS, dtype=jnp.int32)
    here = takes[:, None, :] & (position[None, None, :] == slots[None, :, None])
    return jnp.sum(jnp.where(here, ids, 0), axis=2), jnp.sum(takes.astype(jnp.int32), axis=1)


def body(coupling, pivot_inverse, pivots, trailing, sketch, extend_map, parent_of, parent_base):
    picks, counts = family(parent_of)
    tall, wide = level(
        picks, counts, coupling[0], pivot_inverse[0], pivots, trailing[0], sketch[0, 0], extend_map,
        parent_base.shape[1],
    )
    return place(tall, wide, parent_base[0])[None]


def solution(mesh):
    placed = (
        P("front", "panel", None),
        P("front", "panel", None),
        P("front", None),
        P("front", "panel", None),
        P("front", "panel", None, None, None),
        P(),
        P(),
        P("front", "panel", None),
    )
    return jax.shard_map(
        body, mesh=mesh, in_specs=placed, out_specs=P("front", "panel", None), check_vma=False
    )
```

time: 147 us -> 120 us (0.82)
  Pallas kernels: 141 us -> 116 us
  local copies, waits for them, and re-layouts: 3 us -> 0.7 us
    pallas_call x4 -> x2, Pallas kernels: 141 us -> 116 us  [the longest x1 112 us: level(): pl.pallas_call(functools.partial(level_kernel, steps), in_specs=[pl.Block...]
    unnamed x6 -> x0, local copies, waits for them, and re-layouts: 1.59 us -> none
where the time goes in v2:
time: 120 us
  Pallas kernels  116 us (97%)
  other arithmetic  2.25 us (2%)
    pallas_call x1, Pallas kernels, level(): pl.pallas_call(functools.partial(level_kernel, steps), in_specs=[pl.Block...  112 us
    pallas_call x1, Pallas kernels, place(): pl.pallas_call(functools.partial(place_kernel, parts), in_specs=[hbm] * 3...  4.46 us

profile of v2, /device:TPU:2, one launch (start us, length us, event | category | flops | bytes accessed | tf_op | source)
XLA Modules:
  0.0 119.5 jit_solution(1038821660017887486)
XLA Ops:
  0.0 1.4 %convert_reduce_fusion = (s32[32]{0:T(128)}, s32[32]{0:T(128)S(1)}) fusion(s32[32]{0:T(128)} %param.14), kind=kLoop, calls=%fused_computation.1 | loop fusion | flops 8128 | bytes 384 | tf_op jit(solution)/shard_map/reduce_sum | solution.py:559
  1.4 0.7 iota_compare_fusion.1
  2.1 0.2 select_reduce_fusion
  2.3 0.7 copy.9.picks
  3.0 111.9 %level.1 = (bf16[8,128,512]{2,1,0:T(8,128)(2,1)}, bf16[8,128,512]{2,1,0:T(8,128)(2,1)}) custom-call(s32[32,4]{1,0:T(8,128)} %copy.9.picks, s32[32]{0:T(128)} %get-tuple-element.9.counts, bf16[256,2048]{1,0:T(8,128)(2,1)} %bitcast.8, bf16[256,2048]{1,0:T(8,128)(2,1)} %bitcast.9, f32[1,2048]{1,0:T(1,128)} %pivots_ref.1, f32[256,2048]{1,0:T(8,128)} %bitcast.7, ...), custom_call_target="tpu_custom_call" | custom-call | tf_op jit(solution)/shard_map/level/pallas_call | solution.py:290
  114.9 4.5 %place.1 = bf16[512,4096]{1,0:T(8,128)(2,1)} custom-call(bf16[8,128,512]{2,1,0:T(8,128)(2,1)} %get-tuple-element.7.tall_hbm, bf16[8,128,512]{2,1,0:T(8,128)(2,1)} %get-tuple-element.8.wide_hbm, bf16[512,4096]{1,0:T(8,128)(2,1)} %bitcast.6), custom_call_target="tpu_custom_call" | custom-call | tf_op jit(solution)/shard_map/place/pallas_call | solution.py:540
  (1 shorter events, 0.0 us)

commit v3 on v2

--- a/solution.py
+++ b/solution.py
@@ -18,7 +18,7 @@
     )
 
 
-def level_kernel(steps, picks, counts, coupling_hbm, inverse_hbm, pivots_ref, trailing_hbm, omega_hbm, maps_hbm, tall_hbm, wide_hbm,
+def level_kernel(steps, picks, coupling_hbm, inverse_hbm, pivots_ref, trailing_hbm, omega_hbm, maps_hbm, tall_hbm, wide_hbm,
                  coupling_ref, inverses, factors, scaled_ref, schur_ref, omega_ref,
                  maps_ref, spots_ref, own_ref, send_sem, recv_sem, local_sem, staged, *rest):
     panel = lax.axis_index("panel")
@@ -183,7 +183,7 @@
     def spots(s, block, size):
         front = lax.axis_index("front")
         lanes = pl.ds(pl.multiple_of(block * rows, rows), rows)
-        where = jnp.where(s < counts[front], maps_ref[pl.ds(picks[front, s], 1), lanes], -1)
+        where = jnp.where(s < picks[front, MAXKIDS], maps_ref[pl.ds(picks[front, s], 1), lanes], -1)
         ids = lax.broadcasted_iota(jnp.int32, (size, rows), 0)
         return jnp.where(where == ids, 1.0, 0.0).astype(jnp.bfloat16)
 
@@ -248,6 +248,7 @@
     far_factor(3)
     squeeze(3, between=first_hops)
     ex.split_start(3)
+    scatter(0)
     ex.ring_start(3)
     ex.ring_step(1, 2)
     ex.ring_step(2, 2)
@@ -258,12 +259,11 @@
     for g in (1, 2):
         ex.ring_end(g)
         ex.pick_start(g)
-    scatter(0)
     ex.ring_step(3, 3)
+    ex.ring_end(3)
+    ex.pick_start(3)
     scatter(1)
     scatter(2)
-    ex.ring_end(3)
-    ex.pick_start(3)
     scatter(3)
     for g in range(4):
         ex.drain(g)
@@ -279,7 +279,7 @@
     lax.fori_loop(0, steps, drain, 0)
 
 
-def level(picks, counts, coupling, pivot_inverse, pivots, trailing, omega, maps, height):
+def level(picks, coupling, pivot_inverse, pivots, trailing, omega, maps, height):
     rows, cols = coupling.shape
     tiles, rank, tile = omega.shape
     pieces = cols // rows
@@ -289,7 +289,7 @@
     spread = (tiles, MAXKIDS * rank, height)
     return pl.pallas_call(
         functools.partial(level_kernel, steps),
-        in_specs=[pl.BlockSpec(memory_space=pltpu.SMEM)] * 2 + [hbm, hbm, vmem, hbm, hbm, hbm],
+        in_specs=[pl.BlockSpec(memory_space=pltpu.SMEM), hbm, hbm, vmem, hbm, hbm, hbm],
         out_specs=(hbm, hbm),
         out_shape=(jax.ShapeDtypeStruct(spread, jnp.bfloat16),) * 2,
         scratch_shapes=[
@@ -310,7 +310,7 @@
         compiler_params=pltpu.CompilerParams(
             collective_id=0, has_side_effects=True, vmem_limit_bytes=60 * 1024 * 1024
         ),
-    )(picks, counts, coupling, pivot_inverse, pivots, trailing, omega, maps)
+    )(picks, coupling, pivot_inverse, pivots, trailing, omega, maps)
 
 
 def halves(value):
@@ -549,20 +549,40 @@
     )(tall, wide, base)
 
 
+def family_kernel(parent_of, picks):
+    fronts = parent_of.shape[0]
+
+    def clear(q, carry):
+        for s in range(MAXKIDS + 1):
+            picks[q, s] = 0
+        return carry
+
+    def put(front, carry):
+        parent = parent_of[front]
+        count = picks[parent, MAXKIDS]
+        picks[parent, count] = front
+        picks[parent, MAXKIDS] = count + 1
+        return carry
+
+    lax.fori_loop(0, fronts, clear, 0, unroll=4)
+    lax.fori_loop(0, fronts, put, 0)
+
+
 def family(parent_of):
-    ids = jnp.arange(parent_of.shape[0], dtype=jnp.int32)
-    earlier = (parent_of[:, None] == parent_of[None, :]) & (ids[None, :] < ids[:, None])
-    position = jnp.sum(earlier.astype(jnp.int32), axis=1)
-    takes = parent_of[None, :] == ids[:, None]
-    slots = jnp.arange(MAXKIDS, dtype=jnp.int32)
-    here = takes[:, None, :] & (position[None, None, :] == slots[None, :, None])
-    return jnp.sum(jnp.where(here, ids, 0), axis=2), jnp.sum(takes.astype(jnp.int32), axis=1)
+    smem = pl.BlockSpec(memory_space=pltpu.SMEM)
+    return pl.pallas_call(
+        family_kernel,
+        in_specs=[smem],
+        out_specs=smem,
+        out_shape=jax.ShapeDtypeStruct((parent_of.shape[0], MAXKIDS + 1), jnp.int32),
+        name="family",
+    )(parent_of)
 
 
 def body(coupling, pivot_inverse, pivots, trailing, sketch, extend_map, parent_of, parent_base):
-    picks, counts = family(parent_of)
+    picks = family(parent_of)
     tall, wide = level(
-        picks, counts, coupling[0], pivot_inverse[0], pivots, trailing[0], sketch[0, 0], extend_map,
+        picks, coupling[0], pivot_inverse[0], pivots, trailing[0], sketch[0, 0], extend_map,
         parent_base.shape[1],
     )
     return place(tall, wide, parent_base[0])[None]

time: 120 us -> 117 us (0.975)
  other arithmetic: 2.25 us -> 0 us
    pallas_call x0 -> x1, Pallas kernels: none -> 2.07 us  [family(): pl.pallas_call(family_kernel, in_specs=[smem], out_specs=smem, out_shape=...]
    pallas_call x1, Pallas kernels: 112 us -> 110 us  [level(): pl.pallas_call(functools.partial(level_kernel, steps), in_specs=[pl.Block...]
    reduce_sum x2 -> x0, other arithmetic: 1.58 us -> none  [the longest x1 1.43 us: family(): jnp.sum(takes.astype(jnp.int32), axis=1)]
where the time goes in v3:
time: 117 us
  Pallas kernels  117 us (100%)
    pallas_call x1, Pallas kernels, level(): pl.pallas_call(functools.partial(level_kernel, steps), in_specs=[pl.Block...  110 us
    pallas_call x1, Pallas kernels, place(): pl.pallas_call(functools.partial(place_kernel, parts), in_specs=[hbm] * 3...  4.46 us

profile of v3, /device:TPU:2, one launch (start us, length us, event | category | flops | bytes accessed | tf_op | source)
XLA Modules:
  0.0 116.7 jit_solution(15700641380185673713)
XLA Ops:
  0.0 2.1 %family.1.picks = s32[32,5]{1,0:T(8,128)} custom-call(s32[32]{0:T(128)} %parent_of.1), custom_call_target="tpu_custom_call" | custom-call | tf_op jit(solution)/shard_map/family/pallas_call | solution.py:573
  2.1 110.0 %level.1 = (bf16[8,128,512]{2,1,0:T(8,128)(2,1)}, bf16[8,128,512]{2,1,0:T(8,128)(2,1)}) custom-call(s32[32,5]{1,0:T(8,128)} %family.1.picks, bf16[256,2048]{1,0:T(8,128)(2,1)} %bitcast.8, bf16[256,2048]{1,0:T(8,128)(2,1)} %bitcast.9, f32[1,2048]{1,0:T(1,128)} %pivots_ref.1, f32[256,2048]{1,0:T(8,128)} %bitcast.7, f32[8,32,256]{2,1,0:T(8,128)} %bitcast.10, ...), custom_call_target="tpu_custom_call" | custom-call | tf_op jit(solution)/shard_map/level/pallas_call | solution.py:290
  112.1 4.5 %place.1 = bf16[512,4096]{1,0:T(8,128)(2,1)} custom-call(bf16[8,128,512]{2,1,0:T(8,128)(2,1)} %get-tuple-element.7.tall_hbm, bf16[8,128,512]{2,1,0:T(8,128)(2,1)} %get-tuple-element.8.wide_hbm, bf16[512,4096]{1,0:T(8,128)(2,1)} %bitcast.6), custom_call_target="tpu_custom_call" | custom-call | tf_op jit(solution)/shard_map/place/pallas_call | solution.py:540
